TPU v7x, 32 devices: a whole 2x2x4 slice. The times are simulated.
32 devices in a mesh: orb: 16 (over z, y, core), grid: 2 (over x).
Axes of the slice: x: 2, y: 2, z: 4, core: 2. Of those that a mesh axis runs over, the one named last changes fastest.
Arguments:
- orbitals: bfloat16 [32, 11520], P('orb', 'grid'), may hold values from -1.5 to 1.5
- occupation: bfloat16 [32], P('orb'), may hold values from 0.29882812 to 1
Outputs:
- potentials: float32 [32, 11520], P('orb', 'grid')
- projectors: float32 [32, 11520], P('orb', 'grid')
All inputs are finite; a program needn't handle non-finite values.
Results may differ from a plain program's by a relative error of at most 0.0025.
Values may be sent and summed in bfloat16 or wider, within the bound.
No kernel may reach another device: no remote copies, remote signals or barrier semaphores. Data moves between devices by JAX's collectives and lax.ppermute only.
A program may use at most 64 MiB of HBM per device.

v0:
```python
import math
import jax
import jax.numpy as jnp
from jax import lax
from jax.sharding import PartitionSpec as P

NX = 20
NY = 24
NZ = 24
NPTS = 11520


def hartley_table(length):
    index = jnp.arange(length, dtype=jnp.int32)
    product = index[:, None] * index[None, :] % length
    angle = 2.0 * math.pi / length * product.astype(jnp.float32)
    return (jnp.cos(angle) + jnp.sin(angle)).astype(jnp.bfloat16)


def signed_square(length):
    index = jnp.arange(length, dtype=jnp.int32)
    signed = jnp.where(index <= length // 2, index, index - length).astype(jnp.float32)
    return (2.0 * math.pi * signed / length) ** 2


def coulomb_kernel(size_x, size_y, size_z):
    total = (
        signed_square(size_x)[:, None, None]
        + signed_square(size_y)[None, :, None]
        + signed_square(size_z)[None, None, :]
    )
    safe = jnp.where(total > 0, total, 1.0)
    return jnp.where(total > 0, 1.0 / safe, 0.0) / (size_x * size_y * size_z)


def solve_pairs(density, table_x, table_y, table_z, kernel):
    section = jnp.einsum(
        "ax,pxyz->payz", table_x, density, preferred_element_type=jnp.float32
    ).astype(jnp.bfloat16)
    section = jnp.einsum(
        "by,pxyz->pxbz", table_y, section, preferred_element_type=jnp.float32
    ).astype(jnp.bfloat16)
    spectrum = jnp.einsum("cz,pxyz->pxyc", table_z, section, preferred_element_type=jnp.float32)
    section = (spectrum * kernel).astype(jnp.bfloat16)
    section = jnp.einsum(
        "cz,pxyz->pxyc", table_z, section, preferred_element_type=jnp.float32
    ).astype(jnp.bfloat16)
    section = jnp.einsum(
        "by,pxyz->pxbz", table_y, section, preferred_element_type=jnp.float32
    ).astype(jnp.bfloat16)
    return jnp.einsum("ax,pxyz->payz", table_x, section, preferred_element_type=jnp.float32)


def pair_folder(targets, running, pieces):
    table_x = hartley_table(NX)
    table_y = hartley_table(NY)
    table_z = hartley_table(NZ)
    kernel = coulomb_kernel(NX, NY, NZ)
    target_rows = targets.astype(jnp.float32)
    target_count = targets.shape[0]
    block, block_weight = pieces
    rows = block.shape[0]
    group = math.gcd(rows, 64)
    blocks = block.reshape(rows // group, group, NPTS)
    weights = block_weight.astype(jnp.float32).reshape(rows // group, group)

    def accumulate(totals, inputs):
        sources, source_weight = inputs
        source_rows = sources.astype(jnp.float32)
        density = (target_rows[:, None, :] * source_rows[None, :, :]).astype(jnp.bfloat16)
        density = density.reshape(target_count * group, NX, NY, NZ)
        potential = solve_pairs(density, table_x, table_y, table_z, kernel).reshape(
            target_count, group, NPTS
        )
        weighted = source_weight[None, :, None] * potential * source_rows[None, :, :]
        return (totals - jnp.sum(weighted, axis=1), None)

    result, unused = lax.scan(accumulate, running, (blocks, weights))
    return result


def on_device(orbitals, occupation):
    own_count = orbitals.shape[0]
    per_device = own_count // lax.axis_size("grid")
    empty = jnp.zeros((per_device, NPTS), jnp.float32)
    whole = lax.all_gather(orbitals, "grid", axis=1, tiled=True)
    targets = lax.dynamic_slice_in_dim(whole, lax.axis_index("grid") * per_device, per_device, 0)
    totals = pair_folder(
        targets,
        empty,
        (
            lax.all_gather(whole, "orb", axis=0, tiled=True),
            lax.all_gather(occupation, "orb", axis=0, tiled=True),
        ),
    )
    potentials = lax.all_to_all(totals, "grid", split_axis=1, concat_axis=0, tiled=True)
    source_points, potential_points = (
        lax.all_to_all(
            orbitals.astype(jnp.float32), "orb", split_axis=1, concat_axis=0, tiled=True
        ),
        lax.all_to_all(potentials, "orb", split_axis=1, concat_axis=0, tiled=True),
    )
    partial_gram = (
        lax.dot_general(
            source_points,
            potential_points,
            (((1,), (1,)), ((), ())),
            precision=lax.Precision.HIGHEST,
        )
        / NPTS
    )
    gram = lax.psum(partial_gram, ("orb", "grid"))
    factor = jnp.linalg.cholesky(-gram)
    identity = jnp.eye(gram.shape[0], dtype=jnp.float32)
    inverse = lax.linalg.triangular_solve(factor, identity, left_side=True, lower=True)
    projector_points = jnp.dot(inverse, potential_points, precision=lax.Precision.HIGHEST)
    projectors = lax.all_to_all(projector_points, "orb", split_axis=0, concat_axis=1, tiled=True)
    return (potentials, projectors)


def solution(mesh):
    placed = (P("orb", "grid"), P("orb"))
    return jax.shard_map(
        on_device,
        mesh=mesh,
        in_specs=placed,
        out_specs=(P("orb", "grid"), P("orb", "grid")),
        check_vma=False,
    )
```

profile of v0, /device:TPU:0, one launch (start us, length us, event | category | flops | bytes accessed | tf_op | source)
XLA Modules:
  0.0 226.1 jit_solution(919936937522886090)
XLA Ops:
  0.7 5.7 %all_gather.10 = bf16[2,11520]{1,0:T(2,128)(2,1)S(1)} all-gather(bf16[2,5760]{1,0:T(2,128)(2,1)} %param.2), channel_id=1, replica_groups=mesh['orb'=16,'grid'=2] {'grid'}, dimensions={1}, use_global_device_ids=true | all-gather | bytes 69120 | tf_op jit(solution)/shard_map/all_gather | solution.py:86
  6.3 24.3 %all-gather = bf16[16,2,11520]{2,1,0:T(2,128)(2,1)S(1)} all-gather(bf16[1,2,11520]{2,1,0:T(2,128)(2,1)S(1)} %bitcast.58), channel_id=1, replica_groups=mesh['orb'=16,'grid'=2] {'orb'}, dimensions={0}, use_global_device_ids=true | all-gather | bytes 783360 | tf_op jit(solution)/shard_map/all_gather | solution.py:92
  30.7 6.4 %reshape.167 = f32[32,20,24,24]{3,2,1,0:T(8,128)} reshape(bf16[16,2,11520]{2,1,0:T(2,128)(2,1)S(1)} %all-gather) | data formatting | bytes 2211840 | tf_op jit(solution)/shard_map/while/body/eval_jaxpr/convert_element_type | solution.py:69
  37.1 1.3 reshape.174
  38.4 0.1 convert_reduce_fusion
  38.6 0.2 reshape.166
  38.8 3.9 %multiply_convert_fusion.1 = bf16[32,20,24,24]{3,2,1,0:T(8,128)(2,1)S(1)} fusion(f32[32,20,24,24]{3,2,1,0:T(8,128)} %reshape.167, f32[20,24,24]{2,1,0:T(8,128)S(1)} %reshape.166), kind=kLoop, calls=%fused_computation.1 | loop fusion | flops 737280 | bytes 2257920 | tf_op jit(solution)/shard_map/while/body/eval_jaxpr/convert_element_type | solution.py:70
  42.6 4.9 %convert_bitcast_fusion = bf16[32,20,24,24]{1,3,2,0:T(8,128)(2,1)} fusion(bf16[32,20,24,24]{3,2,1,0:T(8,128)(2,1)S(1)} %multiply_convert_fusion.1), kind=kOutput, calls=%fused_computation.4 | convolution fusion | flops 15118640 | bytes 1474560 | tf_op jit(solution)/shard_map/while/body/eval_jaxpr/ax,pxyz->payz/dot_general | solution.py:37
  47.5 8.5 %copy.24 = bf16[32,20,24,24]{2,3,1,0:T(8,128)(2,1)} copy(bf16[32,20,24,24]{1,3,2,0:T(8,128)(2,1)} %convert_bitcast_fusion) | data formatting | bytes 1474560 | tf_op jit(solution)/shard_map/while/body/eval_jaxpr/convert_element_type | solution.py:39
  56.0 5.2 %fusion.44 = bf16[32,20,24,24]{3,2,1,0:T(8,128)(2,1)} fusion(bf16[32,20,24,24]{2,3,1,0:T(8,128)(2,1)} %copy.24), kind=kOutput, calls=%fused_computation.53 | convolution fusion | flops 17701056 | bytes 1474560 | tf_op jit(solution)/shard_map/while/body/eval_jaxpr/by,pxyz->pxbz/dot_general | solution.py:40
  61.2 0.1 broadcast_add_fusion
  61.3 0.1 fusion.19
  61.5 7.4 %fusion.2 = bf16[32,20,24,24]{3,2,1,0:T(8,128)(2,1)} fusion(f32[20,24,24]{2,1,0:T(8,128)S(1)} %fusion.19, bf16[32,20,24,24]{3,2,1,0:T(8,128)(2,1)} %fusion.44), kind=kOutput, calls=%fused_computation.5 | convolution fusion | flops 36139392 | bytes 1520640 | tf_op jit(solution)/shard_map/while/body/eval_jaxpr/cz,pxyz->pxyc/dot_general | solution.py:45
  68.9 5.4 %convert_bitcast_fusion.1 = bf16[32,20,24,24]{2,3,1,0:T(8,128)(2,1)} fusion(bf16[32,20,24,24]{3,2,1,0:T(8,128)(2,1)} %fusion.2), kind=kOutput, calls=%fused_computation.8 | convolution fusion | flops 18069696 | bytes 1474560 | tf_op jit(solution)/shard_map/while/body/eval_jaxpr/by,pxyz->pxbz/dot_general | solution.py:48
  74.3 10.1 %copy.27 = bf16[32,20,24,24]{0,1,3,2:T(8,128)(2,1)S(1)} copy(bf16[32,20,24,24]{2,3,1,0:T(8,128)(2,1)} %convert_bitcast_fusion.1) | data formatting | bytes 1474560 | tf_op jit(solution)/shard_map/while/body/eval_jaxpr/convert_element_type | solution.py:50
  84.4 4.0 %convolution_bitcast_fusion = f32[32,20,24,24]{0,1,3,2:T(8,128)} fusion(bf16[32,20,24,24]{0,1,3,2:T(8,128)(2,1)S(1)} %copy.27), kind=kOutput, calls=%fused_computation.13 | convolution fusion | flops 14750000 | bytes 2211840 | tf_op jit(solution)/shard_map/while/body/eval_jaxpr/ax,pxyz->payz/dot_general | solution.py:51
  88.4 0.0 copy-start.3
  88.4 0.0 copy-start.2
  88.4 12.1 %copy.28 = f32[32,20,24,24]{3,2,1,0:T(8,128)} copy(f32[32,20,24,24]{0,1,3,2:T(8,128)} %convolution_bitcast_fusion) | data formatting | bytes 2949120 | tf_op jit(solution)/shard_map/while/body/eval_jaxpr/ax,pxyz->payz/transpose | solution.py:51
  100.5 0.0 copy-done.3
  100.5 0.6 dynamic-slice
  101.8 0.0 copy-done.2
  101.8 0.2 dynamic-update-slice.3
  102.0 0.0 copy-start
  102.0 0.0 copy-start.1
  102.0 6.8 %reshape.165 = f32[32,11520]{1,0:T(8,128)S(1)} reshape(f32[32,20,24,24]{3,2,1,0:T(8,128)} %copy.28) | data formatting | bytes 2949120 | tf_op jit(solution)/shard_map/while/body/eval_jaxpr/reshape | solution.py:72
  108.9 29.9 %all-reduce = bf16[32]{0:T(256)(128)(2,1)S(1)} all-reduce(bf16[32]{0:T(256)(128)(2,1)S(1)} %dynamic-update-slice.3), channel_id=1, replica_groups=mesh['orb'=16,'grid'=2] {'orb'}, use_global_device_ids=true, to_apply=%add | all-reduce | flops 32 | bytes 128
  138.8 0.0 copy-done
  138.8 0.3 multiply_reduce_fusion
  139.1 0.7 sub.25
  139.7 3.3 %all-to-all-start = ((f32[1,2,5760]{2,0,1:T(1,128)}), f32[1,2,5760]{2,0,1:T(1,128)S(1)}, u32[]{:S(2)}, u32[]{:S(2)}) async-start(f32[1,2,5760]{2,0,1:T(1,128)} %sub.25), calls=%async_computation | async-start | bytes 92160 | tf_op jit(solution)/shard_map/all_to_all | solution.py:96
  143.0 0.0 copy-done.1
  143.0 0.1 reshape.168
  143.2 0.6 copy.30
  143.8 3.2 %all-to-all-done = f32[1,2,5760]{2,0,1:T(1,128)S(1)} async-done(((f32[1,2,5760]{2,0,1:T(1,128)}), f32[1,2,5760]{2,0,1:T(1,128)S(1)}, u32[]{:S(2)}, u32[]{:S(2)}) %all-to-all-start) | async-done | bytes 46112 | tf_op jit(solution)/shard_map/all_to_all | solution.py:96
  147.0 3.5 %all-to-all-start.2 = ((f32[2,16,360]{2,0,1:T(2,128)}), f32[2,16,360]{2,0,1:T(2,128)S(1)}, u32[]{:S(2)}, u32[]{:S(2)}) async-start(f32[2,16,360]{2,0,1:T(2,128)} %copy.30), calls=%async_computation.2 | async-start | bytes 98304 | tf_op jit(solution)/shard_map/all_to_all | solution.py:98
  150.5 0.1 reduce.11
  150.7 0.1 all_to_all.54
  150.8 0.6 copy.29
  151.4 5.8 %all-to-all-done.2 = f32[2,16,360]{2,0,1:T(2,128)S(1)} async-done(((f32[2,16,360]{2,0,1:T(2,128)}), f32[2,16,360]{2,0,1:T(2,128)S(1)}, u32[]{:S(2)}, u32[]{:S(2)}) %all-to-all-start.2) | async-done | bytes 46112 | tf_op jit(solution)/shard_map/all_to_all | solution.py:98
  157.3 3.5 %all-to-all-start.1 = ((f32[2,16,360]{2,0,1:T(2,128)}), f32[2,16,360]{2,0,1:T(2,128)S(1)}, u32[]{:S(2)}, u32[]{:S(2)}) async-start(f32[2,16,360]{2,0,1:T(2,128)} %copy.29), calls=%async_computation.1 | async-start | bytes 98304 | tf_op jit(solution)/shard_map/all_to_all | solution.py:101
  160.8 6.7 %all-to-all-done.1 = f32[2,16,360]{2,0,1:T(2,128)S(1)} async-done(((f32[2,16,360]{2,0,1:T(2,128)}), f32[2,16,360]{2,0,1:T(2,128)S(1)}, u32[]{:S(2)}, u32[]{:S(2)}) %all-to-all-start.1) | async-done | bytes 46112 | tf_op jit(solution)/shard_map/all_to_all | solution.py:101
  167.6 0.2 fusion.17
  167.8 38.0 %psum.7 = f32[32,32]{0,1:T(8,128)S(1)} all-reduce(f32[32,32]{0,1:T(8,128)S(1)} %fusion.17), channel_id=1, replica_groups=mesh['orb'=16,'grid'=2] {'orb','grid'}, use_global_device_ids=true, to_apply=%region_1.2 | all-reduce | flops 1024 | bytes 8192 | tf_op jit(solution)/shard_map/psum | solution.py:112
  205.8 0.1 copy.31
  205.8 2.9 %cholesky.17 = f32[32,32]{1,0:T(8,128)S(1)} custom-call(f32[32,32]{1,0:T(8,128)S(1)} %fusion.22), custom_call_target="Cholesky" | custom-call | tf_op jit(solution)/shard_map/jit(cholesky)/cholesky | solution.py:113
  208.8 0.6 compare_reduce_fusion
  209.4 0.7 fusion.21
  210.1 2.4 %custom-call.6 = f32[1,32,32]{1,2,0:T(8,128)S(1)} custom-call(f32[1,32,32]{2,1,0:T(8,128)S(1)} %fusion.21), custom_call_target="InvertDiagBlocksLowerTriangular" | custom-call | tf_op jit(solution)/shard_map/triangular_solve | solution.py:115
  212.5 0.1 copy.32
  212.6 0.2 fusion.23
  212.8 0.2 fusion.88
  213.0 0.6 copy.34
  213.6 5.0 %all-to-all-start.3 = ((f32[16,2,360]{2,1,0:T(2,128)}), f32[16,2,360]{2,1,0:T(2,128)S(1)}, u32[]{:S(2)}, u32[]{:S(2)}) async-start(f32[16,2,360]{2,1,0:T(2,128)} %copy.34), calls=%async_computation.3 | async-start | bytes 98304 | tf_op jit(solution)/shard_map/all_to_all | solution.py:117
  218.6 0.6 copy.48
  219.3 6.1 %all-to-all-done.3 = f32[16,2,360]{2,1,0:T(2,128)S(1)} async-done(((f32[16,2,360]{2,1,0:T(2,128)}), f32[16,2,360]{2,1,0:T(2,128)S(1)}, u32[]{:S(2)}, u32[]{:S(2)}) %all-to-all-start.3) | async-done | bytes 46112 | tf_op jit(solution)/shard_map/all_to_all | solution.py:117
  225.4 0.8 all_to_all.65
  (12 shorter events, 0.2 us)
Async XLA Ops:
  88.4 12.1 %copy-start.3 = (u32[32]{0:T(128)S(1)}, u32[32]{0:T(128)}, u32[]{:S(2)}) copy-start(u32[32]{0:T(128)} %constant.125) | copy-start | bytes 388
  88.4 13.4 %copy-start.2 = (bf16[2]{0:T(256)(128)(2,1)S(1)}, bf16[2]{0:T(256)(128)(2,1)}, u32[]{:S(2)}) copy-start(bf16[2]{0:T(256)(128)(2,1)} %param.3) | copy-start | bytes 16
  102.0 36.7 %copy-start = (f32[32,11520]{1,0:T(8,128)S(1)}, f32[32,11520]{1,0:T(8,128)}, u32[]{:S(2)}) copy-start(f32[32,11520]{1,0:T(8,128)} %reshape.174) | copy-start | bytes 4423684
  102.0 41.0 %copy-start.1 = (bf16[2,5760]{1,0:T(2,128)(2,1)S(1)}, bf16[2,5760]{1,0:T(2,128)(2,1)}, u32[]{:S(2)}) copy-start(bf16[2,5760]{1,0:T(2,128)(2,1)} %param.2) | copy-start | bytes 69124
  139.7 7.3 %all-to-all-start = ((f32[1,2,5760]{2,0,1:T(1,128)}), f32[1,2,5760]{2,0,1:T(1,128)S(1)}, u32[]{:S(2)}, u32[]{:S(2)}) async-start(f32[1,2,5760]{2,0,1:T(1,128)} %sub.25), calls=%async_computation | async-start | bytes 92160 | tf_op jit(solution)/shard_map/all_to_all | solution.py:96
  147.0 10.2 %all-to-all-start.2 = ((f32[2,16,360]{2,0,1:T(2,128)}), f32[2,16,360]{2,0,1:T(2,128)S(1)}, u32[]{:S(2)}, u32[]{:S(2)}) async-start(f32[2,16,360]{2,0,1:T(2,128)} %copy.30), calls=%async_computation.2 | async-start | bytes 98304 | tf_op jit(solution)/shard_map/all_to_all | solution.py:98
  157.3 10.2 %all-to-all-start.1 = ((f32[2,16,360]{2,0,1:T(2,128)}), f32[2,16,360]{2,0,1:T(2,128)S(1)}, u32[]{:S(2)}, u32[]{:S(2)}) async-start(f32[2,16,360]{2,0,1:T(2,128)} %copy.29), calls=%async_computation.1 | async-start | bytes 98304 | tf_op jit(solution)/shard_map/all_to_all | solution.py:101
  213.6 11.8 %all-to-all-start.3 = ((f32[16,2,360]{2,1,0:T(2,128)}), f32[16,2,360]{2,1,0:T(2,128)S(1)}, u32[]{:S(2)}, u32[]{:S(2)}) async-start(f32[16,2,360]{2,1,0:T(2,128)} %copy.34), calls=%async_computation.3 | async-start | bytes 98304 | tf_op jit(solution)/shard_map/all_to_all | solution.py:117
where the time goes:
time: 227 us; the launch traced here: 226 us
  blocking collectives  97.9 us (43%)
  local copies, waits for them, and re-layouts  50.8 us (22%)
  matrix products  27.5 us (12%)
  waiting for transfers between devices  21.9 us (10%)
  starting transfers between devices  15.3 us (7%)
  other arithmetic  11.4 us (5%)
    psum x1, blocking collectives, on_device(): gram = lax.psum(partial_gram, ('orb', 'grid'))  38 us
    unnamed x1, blocking collectives  29.9 us
    all_gather x1, blocking collectives, on_device(): lax.all_gather(whole, 'orb', axis=0, tiled=True)  24.3 us
    transpose x1, local copies, waits for them, and re-layouts, solve_pairs(): jnp.einsum('ax,pxyz->payz', table_x, section, preferred_element_type=jnp....  12.1 us
    dot_general x2, matrix products, solve_pairs(): jnp.einsum('by,pxyz->pxbz', table_y, section, preferred_element_type=jnp....  10.6 us
    convert_element_type x1, local copies, waits for them, and re-layouts, solve_pairs(): section = jnp.einsum('by,pxyz->pxbz', table_y, section, preferred_element...  10.1 us
    convert_element_type x1, local copies, waits for them, and re-layouts, solve_pairs(): section = jnp.einsum('ax,pxyz->payz', table_x, density, preferred_element...  8.51 us
    convert_element_type x2, local copies, waits for them, and re-layouts, accumulate(): source_rows = sources.astype(jnp.float32)  7.76 us
  transfers between devices with their start and end apart: 4, of which 4 were waited for; matrix products, arithmetic and copies ran while one was open for 1% of the time, Pallas kernels for 0%

commit v1 on v0

--- a/solution.py
+++ b/solution.py
@@ -109,7 +109,8 @@
         )
         / NPTS
     )
-    gram = lax.psum(partial_gram, ("orb", "grid"))
+    parts = lax.all_gather(partial_gram, ("orb", "grid"))
+    gram = jnp.sum(parts, axis=0)
     factor = jnp.linalg.cholesky(-gram)
     identity = jnp.eye(gram.shape[0], dtype=jnp.float32)
     inverse = lax.linalg.triangular_solve(factor, identity, left_side=True, lower=True)

time: 227 us -> 254 us (1.12)
  blocking collectives: 97.9 us -> 126 us
    all_gather x0 -> x1, blocking collectives: none -> 66.3 us  [on_device(): parts = lax.all_gather(partial_gram, ('orb', 'grid'))]
    psum x1 -> x0, blocking collectives: 38 us -> none  [on_device(): gram = lax.psum(partial_gram, ('orb', 'grid'))]
where the time goes in v1:
time: 254 us; the launch traced here: 253 us
  blocking collectives  126 us (50%)
  local copies, waits for them, and re-layouts  51 us (20%)
  matrix products  27.5 us (11%)
  waiting for transfers between devices  21.8 us (9%)
  starting transfers between devices  13.8 us (5%)
  other arithmetic  11.4 us (4%)
    all_gather x1, blocking collectives, on_device(): parts = lax.all_gather(partial_gram, ('orb', 'grid'))  66.3 us
    unnamed x1, blocking collectives  29.9 us
    all_gather x1, blocking collectives, on_device(): lax.all_gather(whole, 'orb', axis=0, tiled=True)  24.3 us
    transpose x1, local copies, waits for them, and re-layouts, solve_pairs(): jnp.einsum('ax,pxyz->payz', table_x, section, preferred_element_type=jnp....  12.1 us
    dot_general x2, matrix products, solve_pairs(): jnp.einsum('by,pxyz->pxbz', table_y, section, preferred_element_type=jnp....  10.6 us
    convert_element_type x1, local copies, waits for them, and re-layouts, solve_pairs(): section = jnp.einsum('by,pxyz->pxbz', table_y, section, preferred_element...  10.1 us
    convert_element_type x1, local copies, waits for them, and re-layouts, solve_pairs(): section = jnp.einsum('ax,pxyz->payz', table_x, density, preferred_element...  8.51 us
    convert_element_type x2, local copies, waits for them, and re-layouts, accumulate(): source_rows = sources.astype(jnp.float32)  7.76 us
  transfers between devices with their start and end apart: 4, of which 4 were waited for; matrix products, arithmetic and copies ran while one was open for 1% of the time, Pallas kernels for 0%

profile of v1, /device:TPU:0, one launch (start us, length us, event | category | flops | bytes accessed | tf_op | source)
XLA Modules:
  0.0 253.1 jit_solution(5391506182061745175)
XLA Ops:
  0.7 5.7 %all_gather.16 = bf16[2,11520]{1,0:T(2,128)(2,1)S(1)} all-gather(bf16[2,5760]{1,0:T(2,128)(2,1)} %param.2), channel_id=1, replica_groups=mesh['orb'=16,'grid'=2] {'grid'}, dimensions={1}, use_global_device_ids=true | all-gather | bytes 69120 | tf_op jit(solution)/shard_map/all_gather | solution.py:86
  6.3 24.3 %all-gather.1 = bf16[16,2,11520]{2,1,0:T(2,128)(2,1)S(1)} all-gather(bf16[1,2,11520]{2,1,0:T(2,128)(2,1)S(1)} %bitcast.60), channel_id=1, replica_groups=mesh['orb'=16,'grid'=2] {'orb'}, dimensions={0}, use_global_device_ids=true | all-gather | bytes 783360 | tf_op jit(solution)/shard_map/all_gather | solution.py:92
  30.7 6.4 %reshape.167 = f32[32,20,24,24]{3,2,1,0:T(8,128)} reshape(bf16[16,2,11520]{2,1,0:T(2,128)(2,1)S(1)} %all-gather.1) | data formatting | bytes 2211840 | tf_op jit(solution)/shard_map/while/body/eval_jaxpr/convert_element_type | solution.py:69
  37.1 1.3 reshape.175
  38.4 0.1 convert_reduce_fusion
  38.6 0.2 reshape.166
  38.8 3.9 %multiply_convert_fusion.1 = bf16[32,20,24,24]{3,2,1,0:T(8,128)(2,1)S(1)} fusion(f32[32,20,24,24]{3,2,1,0:T(8,128)} %reshape.167, f32[20,24,24]{2,1,0:T(8,128)S(1)} %reshape.166), kind=kLoop, calls=%fused_computation.1 | loop fusion | flops 737280 | bytes 2257920 | tf_op jit(solution)/shard_map/while/body/eval_jaxpr/convert_element_type | solution.py:70
  42.6 4.9 %convert_bitcast_fusion = bf16[32,20,24,24]{1,3,2,0:T(8,128)(2,1)} fusion(bf16[32,20,24,24]{3,2,1,0:T(8,128)(2,1)S(1)} %multiply_convert_fusion.1), kind=kOutput, calls=%fused_computation.4 | convolution fusion | flops 15118640 | bytes 1474560 | tf_op jit(solution)/shard_map/while/body/eval_jaxpr/ax,pxyz->payz/dot_general | solution.py:37
  47.5 8.5 %copy.39 = bf16[32,20,24,24]{2,3,1,0:T(8,128)(2,1)} copy(bf16[32,20,24,24]{1,3,2,0:T(8,128)(2,1)} %convert_bitcast_fusion) | data formatting | bytes 1474560 | tf_op jit(solution)/shard_map/while/body/eval_jaxpr/convert_element_type | solution.py:39
  56.0 5.2 %fusion.44 = bf16[32,20,24,24]{3,2,1,0:T(8,128)(2,1)} fusion(bf16[32,20,24,24]{2,3,1,0:T(8,128)(2,1)} %copy.39), kind=kOutput, calls=%fused_computation.53 | convolution fusion | flops 17701056 | bytes 1474560 | tf_op jit(solution)/shard_map/while/body/eval_jaxpr/by,pxyz->pxbz/dot_general | solution.py:40
  61.2 0.1 broadcast_add_fusion
  61.3 0.1 fusion.19
  61.5 7.4 %fusion.2 = bf16[32,20,24,24]{3,2,1,0:T(8,128)(2,1)} fusion(f32[20,24,24]{2,1,0:T(8,128)S(1)} %fusion.19, bf16[32,20,24,24]{3,2,1,0:T(8,128)(2,1)} %fusion.44), kind=kOutput, calls=%fused_computation.5 | convolution fusion | flops 36139392 | bytes 1520640 | tf_op jit(solution)/shard_map/while/body/eval_jaxpr/cz,pxyz->pxyc/dot_general | solution.py:45
  68.9 5.4 %convert_bitcast_fusion.1 = bf16[32,20,24,24]{2,3,1,0:T(8,128)(2,1)} fusion(bf16[32,20,24,24]{3,2,1,0:T(8,128)(2,1)} %fusion.2), kind=kOutput, calls=%fused_computation.8 | convolution fusion | flops 18069696 | bytes 1474560 | tf_op jit(solution)/shard_map/while/body/eval_jaxpr/by,pxyz->pxbz/dot_general | solution.py:48
  74.3 10.1 %copy.42 = bf16[32,20,24,24]{0,1,3,2:T(8,128)(2,1)S(1)} copy(bf16[32,20,24,24]{2,3,1,0:T(8,128)(2,1)} %convert_bitcast_fusion.1) | data formatting | bytes 1474560 | tf_op jit(solution)/shard_map/while/body/eval_jaxpr/convert_element_type | solution.py:50
  84.4 4.0 %convolution_bitcast_fusion = f32[32,20,24,24]{0,1,3,2:T(8,128)} fusion(bf16[32,20,24,24]{0,1,3,2:T(8,128)(2,1)S(1)} %copy.42), kind=kOutput, calls=%fused_computation.13 | convolution fusion | flops 14750000 | bytes 2211840 | tf_op jit(solution)/shard_map/while/body/eval_jaxpr/ax,pxyz->payz/dot_general | solution.py:51
  88.4 0.0 copy-start.3
  88.4 0.0 copy-start.2
  88.4 12.1 %copy.43 = f32[32,20,24,24]{3,2,1,0:T(8,128)} copy(f32[32,20,24,24]{0,1,3,2:T(8,128)} %convolution_bitcast_fusion) | data formatting | bytes 2949120 | tf_op jit(solution)/shard_map/while/body/eval_jaxpr/ax,pxyz->payz/transpose | solution.py:51
  100.5 0.0 copy-done.3
  100.5 0.6 dynamic-slice
  101.8 0.0 copy-done.2
  101.8 0.2 dynamic-update-slice.3
  102.0 0.0 copy-start
  102.0 0.0 copy-start.1
  102.0 6.8 %reshape.165 = f32[32,11520]{1,0:T(8,128)S(1)} reshape(f32[32,20,24,24]{3,2,1,0:T(8,128)} %copy.43) | data formatting | bytes 2949120 | tf_op jit(solution)/shard_map/while/body/eval_jaxpr/reshape | solution.py:72
  108.9 29.9 %all-reduce = bf16[32]{0:T(256)(128)(2,1)S(1)} all-reduce(bf16[32]{0:T(256)(128)(2,1)S(1)} %dynamic-update-slice.3), channel_id=1, replica_groups=mesh['orb'=16,'grid'=2] {'orb'}, use_global_device_ids=true, to_apply=%add | all-reduce | flops 32 | bytes 128
  138.8 0.0 copy-done
  138.8 0.3 multiply_reduce_fusion
  139.1 0.7 sub.25
  139.7 3.3 %all-to-all-start = ((f32[1,2,5760]{2,0,1:T(1,128)}), f32[1,2,5760]{2,0,1:T(1,128)S(1)}, u32[]{:S(2)}, u32[]{:S(2)}) async-start(f32[1,2,5760]{2,0,1:T(1,128)} %sub.25), calls=%async_computation | async-start | bytes 92160 | tf_op jit(solution)/shard_map/all_to_all | solution.py:96
  143.0 0.0 copy-done.1
  143.0 0.1 reshape.168
  143.2 0.6 copy.45
  143.8 3.2 %all-to-all-done = f32[1,2,5760]{2,0,1:T(1,128)S(1)} async-done(((f32[1,2,5760]{2,0,1:T(1,128)}), f32[1,2,5760]{2,0,1:T(1,128)S(1)}, u32[]{:S(2)}, u32[]{:S(2)}) %all-to-all-start) | async-done | bytes 46112 | tf_op jit(solution)/shard_map/all_to_all | solution.py:96
  147.0 3.5 %all-to-all-start.2 = ((f32[2,16,360]{2,0,1:T(2,128)}), f32[2,16,360]{2,0,1:T(2,128)S(1)}, u32[]{:S(2)}, u32[]{:S(2)}) async-start(f32[2,16,360]{2,0,1:T(2,128)} %copy.45), calls=%async_computation.2 | async-start | bytes 98304 | tf_op jit(solution)/shard_map/all_to_all | solution.py:98
  150.5 0.1 reduce.11
  150.7 0.1 all_to_all.54
  150.8 0.6 copy.44
  151.4 5.8 %all-to-all-done.2 = f32[2,16,360]{2,0,1:T(2,128)S(1)} async-done(((f32[2,16,360]{2,0,1:T(2,128)}), f32[2,16,360]{2,0,1:T(2,128)S(1)}, u32[]{:S(2)}, u32[]{:S(2)}) %all-to-all-start.2) | async-done | bytes 46112 | tf_op jit(solution)/shard_map/all_to_all | solution.py:98
  157.3 3.5 %all-to-all-start.1 = ((f32[2,16,360]{2,0,1:T(2,128)}), f32[2,16,360]{2,0,1:T(2,128)S(1)}, u32[]{:S(2)}, u32[]{:S(2)}) async-start(f32[2,16,360]{2,0,1:T(2,128)} %copy.44), calls=%async_computation.1 | async-start | bytes 98304 | tf_op jit(solution)/shard_map/all_to_all | solution.py:101
  160.8 6.7 %all-to-all-done.1 = f32[2,16,360]{2,0,1:T(2,128)S(1)} async-done(((f32[2,16,360]{2,0,1:T(2,128)}), f32[2,16,360]{2,0,1:T(2,128)S(1)}, u32[]{:S(2)}, u32[]{:S(2)}) %all-to-all-start.1) | async-done | bytes 46112 | tf_op jit(solution)/shard_map/all_to_all | solution.py:101
  167.6 0.2 fusion.17
  167.8 0.1 copy.46
  167.8 66.3 %all-gather = f32[1024,32]{1,0:T(8,128)S(1)} all-gather(f32[32,32]{1,0:T(8,128)S(1)} %copy.46), channel_id=2, replica_groups=mesh['orb'=16,'grid'=2] {'orb','grid'}, dimensions={0}, use_global_device_ids=true | all-gather | bytes 135168 | tf_op jit(solution)/shard_map/all_gather | solution.py:112
  234.1 0.1 reduce_sum.20
  234.2 0.1 copy.47
  234.3 0.1 copy.48
  234.4 2.9 %cholesky.17 = f32[32,32]{1,0:T(8,128)S(1)} custom-call(f32[32,32]{1,0:T(8,128)S(1)} %fusion.22), custom_call_target="Cholesky" | custom-call | tf_op jit(solution)/shard_map/jit(cholesky)/cholesky | solution.py:114
  237.3 0.6 compare_reduce_fusion
  238.0 0.7 fusion.21
  238.6 2.4 custom-call.6
  241.1 0.1 copy.49
  241.1 0.2 fusion.23
  241.3 0.2 fusion.88
  241.5 0.6 copy.51
  242.1 3.5 %all-to-all-start.3 = ((f32[16,2,360]{2,1,0:T(2,128)}), f32[16,2,360]{2,1,0:T(2,128)S(1)}, u32[]{:S(2)}, u32[]{:S(2)}) async-start(f32[16,2,360]{2,1,0:T(2,128)} %copy.51), calls=%async_computation.3 | async-start | bytes 98304 | tf_op jit(solution)/shard_map/all_to_all | solution.py:118
  245.6 0.6 copy.65
  246.3 6.1 %all-to-all-done.3 = f32[16,2,360]{2,1,0:T(2,128)S(1)} async-done(((f32[16,2,360]{2,1,0:T(2,128)}), f32[16,2,360]{2,1,0:T(2,128)S(1)}, u32[]{:S(2)}, u32[]{:S(2)}) %all-to-all-start.3) | async-done | bytes 46112 | tf_op jit(solution)/shard_map/all_to_all | solution.py:118
  252.4 0.8 all_to_all.65
  (12 shorter events, 0.2 us)
Async XLA Ops:
  88.4 12.1 %copy-start.3 = (u32[32]{0:T(128)S(1)}, u32[32]{0:T(128)}, u32[]{:S(2)}) copy-start(u32[32]{0:T(128)} %constant.125) | copy-start | bytes 388
  88.4 13.4 %copy-start.2 = (bf16[2]{0:T(256)(128)(2,1)S(1)}, bf16[2]{0:T(256)(128)(2,1)}, u32[]{:S(2)}) copy-start(bf16[2]{0:T(256)(128)(2,1)} %param.3) | copy-start | bytes 16
  102.0 36.7 %copy-start = (f32[32,11520]{1,0:T(8,128)S(1)}, f32[32,11520]{1,0:T(8,128)}, u32[]{:S(2)}) copy-start(f32[32,11520]{1,0:T(8,128)} %reshape.175) | copy-start | bytes 4423684
  102.0 41.0 %copy-start.1 = (bf16[2,5760]{1,0:T(2,128)(2,1)S(1)}, bf16[2,5760]{1,0:T(2,128)(2,1)}, u32[]{:S(2)}) copy-start(bf16[2,5760]{1,0:T(2,128)(2,1)} %param.2) | copy-start | bytes 69124
  139.7 7.3 %all-to-all-start = ((f32[1,2,5760]{2,0,1:T(1,128)}), f32[1,2,5760]{2,0,1:T(1,128)S(1)}, u32[]{:S(2)}, u32[]{:S(2)}) async-start(f32[1,2,5760]{2,0,1:T(1,128)} %sub.25), calls=%async_computation | async-start | bytes 92160 | tf_op jit(solution)/shard_map/all_to_all | solution.py:96
  147.0 10.2 %all-to-all-start.2 = ((f32[2,16,360]{2,0,1:T(2,128)}), f32[2,16,360]{2,0,1:T(2,128)S(1)}, u32[]{:S(2)}, u32[]{:S(2)}) async-start(f32[2,16,360]{2,0,1:T(2,128)} %copy.45), calls=%async_computation.2 | async-start | bytes 98304 | tf_op jit(solution)/shard_map/all_to_all | solution.py:98
  157.3 10.2 %all-to-all-start.1 = ((f32[2,16,360]{2,0,1:T(2,128)}), f32[2,16,360]{2,0,1:T(2,128)S(1)}, u32[]{:S(2)}, u32[]{:S(2)}) async-start(f32[2,16,360]{2,0,1:T(2,128)} %copy.44), calls=%async_computation.1 | async-start | bytes 98304 | tf_op jit(solution)/shard_map/all_to_all | solution.py:101
  242.1 10.2 %all-to-all-start.3 = ((f32[16,2,360]{2,1,0:T(2,128)}), f32[16,2,360]{2,1,0:T(2,128)S(1)}, u32[]{:S(2)}, u32[]{:S(2)}) async-start(f32[16,2,360]{2,1,0:T(2,128)} %copy.51), calls=%async_computation.3 | async-start | bytes 98304 | tf_op jit(solution)/shard_map/all_to_all | solution.py:118
